TPU v7x, 512 devices: a whole 4x8x8 slice. The times are simulated.
512 devices in a mesh: row: 32 (over z, x_hi, core), col: 16 (over y, x_lo).
Axes of the slice: x: 4 (x_hi: 2, x_lo: 2; x = x_hi * 2 + x_lo), y: 8, z: 8, core: 2. Of those that a mesh axis runs over, the one named last changes fastest.
Arguments:
- ancestor: float32 [32, 384, 12288], P(None, 'col', 'row'), may hold values from -6 to 6
- panels: float32 [2, 12288, 512], P(None, ('row', 'col')), may hold values from -0.06 to 0.06
- link_panels: float32 [1, 512, 512], P(None, 'row'), may hold values from -0.25 to 0.25
- diag_inverse: float32 [2, 512, 512], P(None, 'row'), may hold values from -0.25 to 0.25
- blocks: int32 [2, 48], replicated, may hold values from 0 to 95, as said below
Outputs:
- columns: float32 [2, 12288, 512], P(None, ('row', 'col'))
- diagonal: float32 [2, 512, 512], P(None, 'row', 'col')
Inputs may be any that keep to these rules, and one draw needn't show every extreme that they name: Each of the 2 rows names 48 different row blocks.
All inputs are finite; a program needn't handle non-finite values.
Results may differ from a plain program's by a relative error of at most 0.0001.
Values sent between devices are 32-bit elements; how exact they have to be, the bound alone decides.
A program may use at most 64 MiB of HBM per device.

v0:
```python
import jax
import jax.numpy as jnp
from jax import lax
from jax.sharding import Mesh
from jax.sharding import PartitionSpec as P

BLOCK = 128
ROW = ("row_0", "row_1", "row_2")
ROW_COL = ("row_0", "row_1", "row_2", "col")


def joined_along(blocks, dim):
    blocks = jnp.moveaxis(blocks, 0, dim)
    shape = blocks.shape
    return blocks.reshape(*shape[:dim], shape[dim] * shape[dim + 1], *shape[dim + 2 :])


def gather_in_order(shard, axes, turns):
    blocks = shard[None]
    for k in turns:
        blocks = lax.all_gather(blocks, axes[k], axis=0, tiled=True)
    block = [lax.axis_size(axes[k]) for k in reversed(turns)]
    blocks = blocks.reshape(*block, *shard.shape)
    turned = sorted(range(len(turns)), key=lambda place: turns[len(turns) - 1 - place])
    return blocks.transpose(*turned, *range(len(turns), blocks.ndim)).reshape(-1, *shard.shape)


def gather_axes(shard, axes, turns, dim):
    return joined_along(gather_in_order(shard, axes, turns), dim)


def split_up(shard, dim, length):
    before, after = (shard.shape[:dim], shard.shape[dim + 1 :])
    return jnp.moveaxis(shard.reshape(*before, length, -1, *after), dim, 0)


def sum_at_owner(shard, axis, dim):
    blocks = split_up(shard, dim, lax.axis_size(axis))
    arrived = lax.all_to_all(blocks, axis, split_axis=0, concat_axis=0, tiled=True)
    return arrived.sum(axis=0)


def from_everyone(shard, axis):
    length = lax.axis_size(axis)
    return lax.all_to_all(
        jnp.broadcast_to(shard[None], (length, *shard.shape)), axis, 0, 0, tiled=True
    )


def collect(shard, axis, dim):
    return joined_along(from_everyone(shard, axis), dim)


def matmul(left, right):
    return jnp.dot(left, right, precision=lax.Precision.HIGHEST, preferred_element_type=jnp.float32)


def matmul_left_t(left, right):
    return lax.dot_general(
        left,
        right,
        (((0,), (0,)), ((), ())),
        precision=lax.Precision.HIGHEST,
        preferred_element_type=jnp.float32,
    )


def select_rows(values, row_block, chosen):
    hit = jnp.any(row_block[:, None] == chosen[None, :], axis=1)
    return jnp.where(hit[:, None], values, jnp.float32(0.0))


def body(ancestor, panels, link_panels, diag_inverse, blocks):
    row_count = lax.axis_size(ROW)
    col_count = lax.axis_size("col")
    row_index = lax.axis_index(ROW)
    col_index = lax.axis_index("col")
    resident_t = ancestor.reshape(ancestor.shape[0] * ancestor.shape[1], ancestor.shape[2])
    supernodes = panels.shape[0]
    rows_here = panels.shape[1]
    panel_width = panels.shape[2]
    rows_part = panel_width // row_count
    cols_part = panel_width // col_count
    first_row = (row_index * col_count + col_index) * rows_here
    row_block = (first_row + jnp.arange(rows_here, dtype=jnp.int32)) // BLOCK
    masked = jnp.stack(
        [select_rows(panels[number], row_block, blocks[number]) for number in range(supernodes)]
    )
    joined = jnp.transpose(masked, (1, 0, 2)).reshape(rows_here, supernodes * panel_width)
    folded = matmul_left_t(resident_t, gather_axes(joined, ROW, (1, 0, 2), 0))
    summed = sum_at_owner(folded, "col", 0).reshape(rows_here, supernodes, panel_width)
    links_all = lax.all_gather(link_panels, ROW, axis=1, tiled=True)
    global_rows = row_index * rows_part + jnp.arange(rows_part, dtype=jnp.int32)
    lower_keep = jnp.arange(panel_width, dtype=jnp.int32)[None, :] <= global_rows[:, None]
    col_list = []
    diag_list = []
    prev_cols = None
    prev_rows = None
    for supernode in range(supernodes):
        local_panel = masked[supernode]
        product = summed[:, supernode, :]
        if supernode > 0:
            link = links_all[supernode - 1]
        lowered = jnp.where(lower_keep, diag_inverse[supernode], jnp.float32(0.0))
        right_part = lax.dynamic_slice_in_dim(lowered, col_index * cols_part, cols_part, 1)
        share = matmul(lowered.T, right_part)
        if supernode == 0:
            cols_now = -product
            partial_value = -matmul(local_panel.T, cols_now)
        else:
            carried = matmul(prev_cols, link)
            cols_now = -(product + carried)
            partial_value = matmul(carried.T, local_panel) - matmul(local_panel.T, cols_now)
            link_cols = lax.dynamic_slice_in_dim(link, col_index * cols_part, cols_part, 1)
            link_rows = lax.dynamic_slice_in_dim(link, row_index * rows_part, rows_part, 0)
            share = share + matmul(link_rows.T, matmul(prev_rows, link_cols))
        current = lax.dynamic_slice_in_dim(partial_value, col_index * cols_part, cols_part, 1)
        partial_value = lax.dynamic_update_slice_in_dim(
            partial_value, current + share, col_index * cols_part, 1
        )
        column_block = sum_at_owner(partial_value, "col", 1)
        diag_block = sum_at_owner(column_block, ROW, 0)
        if supernode + 1 < supernodes:
            prev_rows = collect(diag_block, "col", 1)
        col_list.append(cols_now)
        diag_list.append(diag_block)
        prev_cols = cols_now
    return (jnp.stack(col_list), jnp.stack(diag_list))


def solution(mesh):
    torus = Mesh(
        mesh.devices.reshape(8, 2, 2, mesh.shape["col"]), ("row_0", "row_1", "row_2", "col")
    )
    return jax.shard_map(
        body,
        mesh=torus,
        in_specs=(
            P(None, "col", ROW),
            P(None, ROW_COL, None),
            P(None, ROW, None),
            P(None, ROW, None),
            P(),
        ),
        out_specs=(P(None, ROW_COL, None), P(None, ROW, "col")),
        check_vma=False,
    )
```

profile of v0, /device:TPU:1, one launch (start us, length us, event | category | flops | bytes accessed | tf_op | source)
XLA Modules:
  0.0 295.9 jit_solution(991701370696724680)
XLA Ops:
  8.1 0.8 slice_bitcast_fusion
  9.1 0.9 slice_select_fusion
  10.1 6.3 %all_gather.12 = f32[2,24,1024]{2,1,0:T(8,128)} all-gather(f32[1,24,1024]{2,1,0:T(8,128)S(1)} %broadcast_in_dim_reshape.3), channel_id=1, replica_groups=mesh['row_0'=8,'row_1'=2,'row_2'=2,'col'=16] {'row_1'}, dimensions={0}, use_global_device_ids=true | all-gather | bytes 294912 | tf_op jit(solution)/shard_map/all_gather | solution.py:21
  16.5 45.2 %all-gather.4.cloned.1.call-done = f32[16,24,1024]{2,1,0:T(8,128)} async-done(((f32[2,24,1024]{2,1,0:T(8,128)}), f32[16,24,1024]{2,1,0:T(8,128)}) %all-gather.4.cloned.1.call-update) | async-done | bytes 1572880 | tf_op jit(solution)/shard_map/all_gather | solution.py:21
  61.7 25.8 %all-gather.6.cloned.1.call-done = f32[32,24,1024]{2,1,0:T(8,128)} async-done(((f32[16,24,1024]{2,1,0:T(8,128)}), f32[32,24,1024]{2,1,0:T(8,128)}) %all-gather.6.cloned.1.call-update) | async-done | bytes 3145744 | tf_op jit(solution)/shard_map/all_gather | solution.py:21
  87.6 2.1 copy.23
  89.7 5.2 %fusion.35 = f32[1024,384]{0,1:T(8,128)} fusion(f32[768,1024]{1,0:T(8,128)S(1)} %bitcast.71, f32[768,384]{1,0:T(8,128)S(1)} %bitcast.70), kind=kOutput, calls=%fused_computation.58 | convolution fusion | flops 3623878656 | bytes 5898240 | tf_op jit(solution)/shard_map/dot_general | solution.py:59
  94.9 6.6 %all-to-all-start = ((f32[16,24,1024]{2,1,0:T(8,128)}), f32[16,24,1024]{2,1,0:T(8,128)S(1)}, u32[]{:S(2)}, u32[]{:S(2)}) async-start(f32[16,24,1024]{2,1,0:T(8,128)} %bitcast.72), calls=%async_computation | async-start | bytes 3145728 | tf_op jit(solution)/shard_map/all_to_all | solution.py:39
  102.2 35.6 %all-to-all-done = f32[16,24,1024]{2,1,0:T(8,128)S(1)} async-done(((f32[16,24,1024]{2,1,0:T(8,128)}), f32[16,24,1024]{2,1,0:T(8,128)S(1)}, u32[]{:S(2)}, u32[]{:S(2)}) %all-to-all-start) | async-done | bytes 1572896 | tf_op jit(solution)/shard_map/all_to_all | solution.py:39
  138.0 2.0 convolution_negate_fusion
  140.0 1.8 fusion.2
  141.8 6.6 %all-to-all-start.1 = ((f32[16,512,32]{1,2,0:T(8,128)}), f32[16,512,32]{1,2,0:T(8,128)S(1)}, u32[]{:S(2)}, u32[]{:S(2)}) async-start(f32[16,512,32]{1,2,0:T(8,128)} %bitcast.17), calls=%async_computation.1 | async-start | bytes 2097152 | tf_op jit(solution)/shard_map/all_to_all | solution.py:39
  148.8 50.5 %all-gather.8.cloned.1.call-done = f32[1,512,512]{2,1,0:T(8,128)} async-done(((f32[1,16,512]{2,1,0:T(8,128)}), f32[1,512,512]{2,1,0:T(8,128)}) %all-gather.8.cloned.1.call-update) | async-done | bytes 1048592 | tf_op jit(solution)/shard_map/all_gather | solution.py:92
  199.3 1.8 fusion.3
  201.4 0.8 reshape.96
  202.2 4.9 %all-to-all-start.2 = ((f32[32,1,512]{2,1,0:T(1,128)}), f32[32,1,512]{2,1,0:T(1,128)S(1)}, u32[]{:S(2)}, u32[]{:S(2)}) async-start(f32[32,1,512]{2,1,0:T(1,128)} %reshape.96), calls=%async_computation.2 | async-start | bytes 131072 | tf_op jit(solution)/shard_map/all_to_all | solution.py:39
  207.1 1.1 fusion.13
  208.2 8.7 %all-to-all-done.2 = f32[32,1,512]{2,1,0:T(1,128)S(1)} async-done(((f32[32,1,512]{2,1,0:T(1,128)}), f32[32,1,512]{2,1,0:T(1,128)S(1)}, u32[]{:S(2)}, u32[]{:S(2)}) %all-to-all-start.2) | async-done | bytes 65568 | tf_op jit(solution)/shard_map/all_to_all | solution.py:39
  217.4 0.8 reduce
  218.4 0.7 reshape.98
  219.1 8.2 %all-to-all-start.3 = ((f32[16,1,512]{2,1,0:T(1,128)}), f32[16,1,512]{2,1,0:T(1,128)S(1)}, u32[]{:S(2)}, u32[]{:S(2)}) async-start(f32[16,1,512]{2,1,0:T(1,128)} %reshape.98), calls=%async_computation.3 | async-start | bytes 65536 | tf_op jit(solution)/shard_map/all_to_all | solution.py:45
  227.3 2.0 convolution_subtract_fusion
  229.3 5.7 %all-to-all-done.3 = f32[16,1,512]{2,1,0:T(1,128)S(1)} async-done(((f32[16,1,512]{2,1,0:T(1,128)}), f32[16,1,512]{2,1,0:T(1,128)S(1)}, u32[]{:S(2)}, u32[]{:S(2)}) %all-to-all-start.3) | async-done | bytes 32800 | tf_op jit(solution)/shard_map/all_to_all | solution.py:45
  235.0 0.7 reduce.1
  236.0 1.3 fusion.5
  237.3 1.7 fusion.1
  239.0 3.7 %all-to-all-start.4 = ((f32[16,512,32]{1,2,0:T(8,128)}), f32[16,512,32]{1,2,0:T(8,128)S(1)}, u32[]{:S(2)}, u32[]{:S(2)}) async-start(f32[16,512,32]{1,2,0:T(8,128)} %bitcast.26), calls=%async_computation.4 | async-start | bytes 2097152 | tf_op jit(solution)/shard_map/all_to_all | solution.py:39
  242.7 24.4 %all-to-all-done.4 = f32[16,512,32]{1,2,0:T(8,128)S(1)} async-done(((f32[16,512,32]{1,2,0:T(8,128)}), f32[16,512,32]{1,2,0:T(8,128)S(1)}, u32[]{:S(2)}, u32[]{:S(2)}) %all-to-all-start.4) | async-done | bytes 1048608 | tf_op jit(solution)/shard_map/all_to_all | solution.py:39
  267.3 0.8 reshape.100
  268.1 8.8 %all-to-all-start.5 = ((f32[32,1,512]{2,1,0:T(1,128)}), f32[32,1,512]{2,1,0:T(1,128)S(1)}, u32[]{:S(2)}, u32[]{:S(2)}) async-start(f32[32,1,512]{2,1,0:T(1,128)} %reshape.100), calls=%async_computation.5 | async-start | bytes 131072 | tf_op jit(solution)/shard_map/all_to_all | solution.py:39
  277.6 9.2 %all-to-all-done.5 = f32[32,1,512]{2,1,0:T(1,128)S(1)} async-done(((f32[32,1,512]{2,1,0:T(1,128)}), f32[32,1,512]{2,1,0:T(1,128)S(1)}, u32[]{:S(2)}, u32[]{:S(2)}) %all-to-all-start.5) | async-done | bytes 65568 | tf_op jit(solution)/shard_map/all_to_all | solution.py:39
  286.8 0.8 reduce.2
  (41 shorter events, 4.5 us)
Async XLA Ops:
  8.0 81.7 %copy-start = (f32[32,24,384]{2,1,0:T(8,128)S(1)}, f32[32,24,384]{2,1,0:T(8,128)}, u32[]{:S(2)}) copy-start(f32[32,24,384]{2,1,0:T(8,128)} %param.5) | copy-start | bytes 3538948
  8.0 53.7 %all-gather.4.cloned.1.call-start = ((), (), s32[]{:S(2)}) async-start(), calls=%async_computation.6 | async-start | bytes 1769472 | tf_op jit(solution)/shard_map/all_gather | solution.py:21
  16.5 71.1 %all-gather.6.cloned.1.call-start = ((), (), s32[]{:S(2)}) async-start(), calls=%async_computation.7 | async-start | bytes 4718592 | tf_op jit(solution)/shard_map/all_gather | solution.py:21
  94.9 7.2 %copy-start.2 = (f32[2,16,512]{2,1,0:T(8,128)S(1)}, f32[2,16,512]{2,1,0:T(8,128)}, u32[]{:S(2)}) copy-start(f32[2,16,512]{2,1,0:T(8,128)} %param.8) | copy-start | bytes 196612
  94.9 42.9 %all-to-all-start = ((f32[16,24,1024]{2,1,0:T(8,128)}), f32[16,24,1024]{2,1,0:T(8,128)S(1)}, u32[]{:S(2)}, u32[]{:S(2)}) async-start(f32[16,24,1024]{2,1,0:T(8,128)} %bitcast.72), calls=%async_computation | async-start | bytes 3145728 | tf_op jit(solution)/shard_map/all_to_all | solution.py:39
  101.5 97.8 %all-gather.8.cloned.1.call-start = ((), (), s32[]{:S(2)}) async-start(), calls=%async_computation.8 | async-start | bytes 1081344 | tf_op jit(solution)/shard_map/all_gather | solution.py:92
  141.8 59.4 %all-to-all-start.1 = ((f32[16,512,32]{1,2,0:T(8,128)}), f32[16,512,32]{1,2,0:T(8,128)S(1)}, u32[]{:S(2)}, u32[]{:S(2)}) async-start(f32[16,512,32]{1,2,0:T(8,128)} %bitcast.17), calls=%async_computation.1 | async-start | bytes 2097152 | tf_op jit(solution)/shard_map/all_to_all | solution.py:39
  148.5 58.6 %copy-start.1 = (f32[2,24,512]{2,1,0:T(8,128)S(1)}, f32[2,24,512]{2,1,0:T(8,128)}, u32[]{:S(2)}) copy-start(f32[2,24,512]{2,1,0:T(8,128)} %param.6) | copy-start | bytes 294916
  202.2 14.7 %all-to-all-start.2 = ((f32[32,1,512]{2,1,0:T(1,128)}), f32[32,1,512]{2,1,0:T(1,128)S(1)}, u32[]{:S(2)}, u32[]{:S(2)}) async-start(f32[32,1,512]{2,1,0:T(1,128)} %reshape.96), calls=%async_computation.2 | async-start | bytes 131072 | tf_op jit(solution)/shard_map/all_to_all | solution.py:39
  219.1 15.9 %all-to-all-start.3 = ((f32[16,1,512]{2,1,0:T(1,128)}), f32[16,1,512]{2,1,0:T(1,128)S(1)}, u32[]{:S(2)}, u32[]{:S(2)}) async-start(f32[16,1,512]{2,1,0:T(1,128)} %reshape.98), calls=%async_computation.3 | async-start | bytes 65536 | tf_op jit(solution)/shard_map/all_to_all | solution.py:45
  239.0 28.1 %all-to-all-start.4 = ((f32[16,512,32]{1,2,0:T(8,128)}), f32[16,512,32]{1,2,0:T(8,128)S(1)}, u32[]{:S(2)}, u32[]{:S(2)}) async-start(f32[16,512,32]{1,2,0:T(8,128)} %bitcast.26), calls=%async_computation.4 | async-start | bytes 2097152 | tf_op jit(solution)/shard_map/all_to_all | solution.py:39
  268.1 18.7 %all-to-all-start.5 = ((f32[32,1,512]{2,1,0:T(1,128)}), f32[32,1,512]{2,1,0:T(1,128)S(1)}, u32[]{:S(2)}, u32[]{:S(2)}) async-start(f32[32,1,512]{2,1,0:T(1,128)} %reshape.100), calls=%async_computation.5 | async-start | bytes 131072 | tf_op jit(solution)/shard_map/all_to_all | solution.py:39
Sparse Core Ops, SparseCore 0:
  16.6 45.0 all-gather.3
  63.8 23.6 all-gather.5
Sparse Core Ops, SparseCore 1:
  105.3 93.9 all-gather.7
where the time goes:
time: 297 us; the launch traced here: 296 us
  waiting for transfers between devices  206 us (69%)
  starting transfers between devices  38.9 us (13%)
  matrix products  17.3 us (6%)
  between operations  15.8 us (5%)
  local copies, waits for them, and re-layouts  6.79 us (2%)
  blocking collectives  6.33 us (2%)
  other arithmetic  5.08 us (2%)
    all_to_all x5, waiting for transfers between devices, sum_at_owner(): lax.all_to_all(blocks, axis, split_axis=0, concat_axis=0, tiled=True)  77.9 us
    all_gather x2, waiting for transfers between devices, gather_in_order(): blocks = lax.all_gather(blocks, axes[k], axis=0, tiled=True)  71 us
    all_gather x1, waiting for transfers between devices, body(): links_all = lax.all_gather(link_panels, ROW, axis=1, tiled=True)  50.5 us
    all_to_all x5, starting transfers between devices, sum_at_owner(): lax.all_to_all(blocks, axis, split_axis=0, concat_axis=0, tiled=True)  30.6 us
    dot_general x8, matrix products, matmul(): jnp.dot(left, right, precision=lax.Precision.HIGHEST, preferred_element_t...  12.1 us
    all_to_all x1, starting transfers between devices, from_everyone(): lax.all_to_all(jnp.broadcast_to(shard[None], (length, *shard.shape)), axi...  8.19 us
    all_gather x1, blocking collectives, gather_in_order(): blocks = lax.all_gather(blocks, axes[k], axis=0, tiled=True)  6.33 us
  transfers between devices with their start and end apart: 9, of which 8 were waited for; matrix products, arithmetic and copies ran while one was open for 3% of the time, Pallas kernels for 0%

commit v1 on v0

--- a/solution.py
+++ b/solution.py
@@ -18,7 +18,9 @@
 def gather_in_order(shard, axes, turns):
     blocks = shard[None]
     for k in turns:
-        blocks = lax.all_gather(blocks, axes[k], axis=0, tiled=True)
+        blocks = jnp.concatenate(
+            lax.all_to_all(jnp.stack([blocks] * lax.axis_size(axes[k])), axes[k], 0, 0), axis=0
+        )
     block = [lax.axis_size(axes[k]) for k in reversed(turns)]
     blocks = blocks.reshape(*block, *shard.shape)
     turned = sorted(range(len(turns)), key=lambda place: turns[len(turns) - 1 - place])

time: 297 us -> 278 us (0.936)
  waiting for transfers between devices: 206 us -> 127 us
  blocking collectives: 6.33 us -> 66.4 us
    all_gather x2 -> x0, waiting for transfers between devices: 71 us -> none  [gather_in_order(): blocks = lax.all_gather(blocks, axes[k], axis=0, tiled=True)]
    all_to_all x0 -> x3, blocking collectives: none -> 66.4 us  [gather_in_order(): lax.all_to_all(jnp.stack([blocks] * lax.axis_size(axes[k])), axes[k], 0, 0)]
    all_gather x1, waiting for transfers between devices: 50.5 us -> 43.7 us  [body(): links_all = lax.all_gather(link_panels, ROW, axis=1, tiled=True)]
    all_gather x1 -> x0, blocking collectives: 6.33 us -> none  [gather_in_order(): blocks = lax.all_gather(blocks, axes[k], axis=0, tiled=True)]
  transfers between devices with their start and end apart: 9 -> 7, of which waited for: 8 -> 6; matrix products, arithmetic and copies ran while one was open for 3% -> 4% of each run, Pallas kernels for 0% -> 0%
where the time goes in v1:
time: 278 us; the launch traced here: 277 us
  waiting for transfers between devices  127 us (46%)
  blocking collectives  66.4 us (24%)
  starting transfers between devices  40.6 us (15%)
  matrix products  17.3 us (6%)
  between operations  14.3 us (5%)
  other arithmetic  5.5 us (2%)
  local copies, waits for them, and re-layouts  5.27 us (2%)
    all_to_all x5, waiting for transfers between devices, sum_at_owner(): lax.all_to_all(blocks, axis, split_axis=0, concat_axis=0, tiled=True)  77.4 us
    all_to_all x3, blocking collectives, gather_in_order(): lax.all_to_all(jnp.stack([blocks] * lax.axis_size(axes[k])), axes[k], 0, 0)  66.4 us
    all_gather x1, waiting for transfers between devices, body(): links_all = lax.all_gather(link_panels, ROW, axis=1, tiled=True)  43.7 us
    all_to_all x5, starting transfers between devices, sum_at_owner(): lax.all_to_all(blocks, axis, split_axis=0, concat_axis=0, tiled=True)  32.4 us
    dot_general x8, matrix products, matmul(): jnp.dot(left, right, precision=lax.Precision.HIGHEST, preferred_element_t...  12.1 us
    all_to_all x1, starting transfers between devices, from_everyone(): lax.all_to_all(jnp.broadcast_to(shard[None], (length, *shard.shape)), axi...  8.1 us
    all_to_all x1, waiting for transfers between devices, from_everyone(): lax.all_to_all(jnp.broadcast_to(shard[None], (length, *shard.shape)), axi...  5.68 us
  transfers between devices with their start and end apart: 7, of which 6 were waited for; matrix products, arithmetic and copies ran while one was open for 4% of the time, Pallas kernels for 0%

profile of v1, /device:TPU:1, one launch (start us, length us, event | category | flops | bytes accessed | tf_op | source)
XLA Modules:
  0.0 276.9 jit_solution(16548071423429158233)
XLA Ops:
  7.2 0.8 slice_bitcast_fusion
  8.2 0.9 slice_select_fusion
  9.3 9.8 %all_to_all.45 = f32[2,1,24,1024]{3,2,1,0:T(8,128)S(1)} all-to-all(f32[2,1,24,1024]{3,2,1,0:T(8,128)S(1)} %pad_maximum_fusion.1), channel_id=1, replica_groups=mesh['row_0'=8,'row_1'=2,'row_2'=2,'col'=16] {'row_1'}, dimensions={0} | all-to-all | bytes 393216 | tf_op jit(solution)/shard_map/all_to_all | solution.py:22
  19.3 46.8 %all_to_all.46 = f32[8,2,24,1024]{3,2,1,0:T(8,128)S(1)} all-to-all(f32[8,2,24,1024]{3,2,1,0:T(8,128)S(1)} %stack.32), channel_id=1, replica_groups=mesh['row_0'=8,'row_1'=2,'row_2'=2,'col'=16] {'row_0'}, dimensions={0} | all-to-all | bytes 3145728 | tf_op jit(solution)/shard_map/all_to_all | solution.py:22
  66.5 9.8 %all_to_all.47 = f32[2,16,24,1024]{3,2,1,0:T(8,128)S(1)} all-to-all(f32[2,16,24,1024]{3,2,1,0:T(8,128)S(1)} %pad_maximum_fusion), channel_id=1, replica_groups=mesh['row_0'=8,'row_1'=2,'row_2'=2,'col'=16] {'row_2'}, dimensions={0} | all-to-all | bytes 6291456 | tf_op jit(solution)/shard_map/all_to_all | solution.py:22
  76.8 5.2 %fusion.35 = f32[1024,384]{0,1:T(8,128)} fusion(f32[768,1024]{1,0:T(8,128)S(1)} %bitcast.74, f32[768,384]{1,0:T(8,128)S(1)} %bitcast.73), kind=kOutput, calls=%fused_computation.60 | convolution fusion | flops 3623878656 | bytes 5898240 | tf_op jit(solution)/shard_map/dot_general | solution.py:61
  82.0 7.1 %all-to-all-start.3 = ((f32[16,24,1024]{2,1,0:T(8,128)}), f32[16,24,1024]{2,1,0:T(8,128)S(1)}, u32[]{:S(2)}, u32[]{:S(2)}) async-start(f32[16,24,1024]{2,1,0:T(8,128)} %bitcast.75), calls=%async_computation.3 | async-start | bytes 3145728 | tf_op jit(solution)/shard_map/all_to_all | solution.py:41
  89.1 0.7 all-gather.2.cloned.1.call-update
  89.9 35.0 %all-to-all-done.3 = f32[16,24,1024]{2,1,0:T(8,128)S(1)} async-done(((f32[16,24,1024]{2,1,0:T(8,128)}), f32[16,24,1024]{2,1,0:T(8,128)S(1)}, u32[]{:S(2)}, u32[]{:S(2)}) %all-to-all-start.3) | async-done | bytes 1572896 | tf_op jit(solution)/shard_map/all_to_all | solution.py:41
  125.2 2.0 convolution_negate_fusion
  127.2 1.8 fusion.2
  129.0 7.1 %all-to-all-start.4 = ((f32[16,512,32]{1,2,0:T(8,128)}), f32[16,512,32]{1,2,0:T(8,128)S(1)}, u32[]{:S(2)}, u32[]{:S(2)}) async-start(f32[16,512,32]{1,2,0:T(8,128)} %bitcast.19), calls=%async_computation.4 | async-start | bytes 2097152 | tf_op jit(solution)/shard_map/all_to_all | solution.py:41
  136.5 43.7 %all-gather.2.cloned.1.call-done = f32[1,512,512]{2,1,0:T(8,128)} async-done(((f32[1,16,512]{2,1,0:T(8,128)}), f32[1,512,512]{2,1,0:T(8,128)}) %all-gather.2.cloned.1.call-update) | async-done | bytes 1048592 | tf_op jit(solution)/shard_map/all_gather | solution.py:94
  180.1 1.8 fusion.3
  182.2 0.8 reshape.94
  183.0 5.8 %all-to-all-start.5 = ((f32[32,1,512]{2,1,0:T(1,128)}), f32[32,1,512]{2,1,0:T(1,128)S(1)}, u32[]{:S(2)}, u32[]{:S(2)}) async-start(f32[32,1,512]{2,1,0:T(1,128)} %reshape.94), calls=%async_computation.5 | async-start | bytes 131072 | tf_op jit(solution)/shard_map/all_to_all | solution.py:41
  188.8 1.1 fusion.13
  189.9 8.7 %all-to-all-done.5 = f32[32,1,512]{2,1,0:T(1,128)S(1)} async-done(((f32[32,1,512]{2,1,0:T(1,128)}), f32[32,1,512]{2,1,0:T(1,128)S(1)}, u32[]{:S(2)}, u32[]{:S(2)}) %all-to-all-start.5) | async-done | bytes 65568 | tf_op jit(solution)/shard_map/all_to_all | solution.py:41
  199.1 0.8 reduce
  200.1 0.7 reshape.96
  200.8 8.1 %all-to-all-start.6 = ((f32[16,1,512]{2,1,0:T(1,128)}), f32[16,1,512]{2,1,0:T(1,128)S(1)}, u32[]{:S(2)}, u32[]{:S(2)}) async-start(f32[16,1,512]{2,1,0:T(1,128)} %reshape.96), calls=%async_computation.6 | async-start | bytes 65536 | tf_op jit(solution)/shard_map/all_to_all | solution.py:47
  208.9 2.0 convolution_subtract_fusion
  211.0 5.7 %all-to-all-done.6 = f32[16,1,512]{2,1,0:T(1,128)S(1)} async-done(((f32[16,1,512]{2,1,0:T(1,128)}), f32[16,1,512]{2,1,0:T(1,128)S(1)}, u32[]{:S(2)}, u32[]{:S(2)}) %all-to-all-start.6) | async-done | bytes 32800 | tf_op jit(solution)/shard_map/all_to_all | solution.py:47
  216.6 0.7 reduce.1
  217.6 1.3 fusion.5
  218.9 1.7 fusion.1
  220.6 3.7 %all-to-all-start.7 = ((f32[16,512,32]{1,2,0:T(8,128)}), f32[16,512,32]{1,2,0:T(8,128)S(1)}, u32[]{:S(2)}, u32[]{:S(2)}) async-start(f32[16,512,32]{1,2,0:T(8,128)} %bitcast.28), calls=%async_computation.7 | async-start | bytes 2097152 | tf_op jit(solution)/shard_map/all_to_all | solution.py:41
  224.3 24.4 %all-to-all-done.7 = f32[16,512,32]{1,2,0:T(8,128)S(1)} async-done(((f32[16,512,32]{1,2,0:T(8,128)}), f32[16,512,32]{1,2,0:T(8,128)S(1)}, u32[]{:S(2)}, u32[]{:S(2)}) %all-to-all-start.7) | async-done | bytes 1048608 | tf_op jit(solution)/shard_map/all_to_all | solution.py:41
  248.9 0.8 reshape.98
  249.7 8.8 %all-to-all-start.8 = ((f32[32,1,512]{2,1,0:T(1,128)}), f32[32,1,512]{2,1,0:T(1,128)S(1)}, u32[]{:S(2)}, u32[]{:S(2)}) async-start(f32[32,1,512]{2,1,0:T(1,128)} %reshape.98), calls=%async_computation.8 | async-start | bytes 131072 | tf_op jit(solution)/shard_map/all_to_all | solution.py:41
  259.2 9.2 %all-to-all-done.8 = f32[32,1,512]{2,1,0:T(1,128)S(1)} async-done(((f32[32,1,512]{2,1,0:T(1,128)}), f32[32,1,512]{2,1,0:T(1,128)S(1)}, u32[]{:S(2)}, u32[]{:S(2)}) %all-to-all-start.8) | async-done | bytes 65568 | tf_op jit(solution)/shard_map/all_to_all | solution.py:41
  268.4 0.8 reduce.2
  (40 shorter events, 4.8 us)
Async XLA Ops:
  7.2 69.6 %copy-start = (f32[32,24,384]{2,1,0:T(8,128)S(1)}, f32[32,24,384]{2,1,0:T(8,128)}, u32[]{:S(2)}) copy-start(f32[32,24,384]{2,1,0:T(8,128)} %param.5) | copy-start | bytes 3538948
  82.0 7.9 %copy-start.2 = (f32[2,16,512]{2,1,0:T(8,128)S(1)}, f32[2,16,512]{2,1,0:T(8,128)}, u32[]{:S(2)}) copy-start(f32[2,16,512]{2,1,0:T(8,128)} %param.8) | copy-start | bytes 196612
  82.0 43.0 %all-to-all-start.3 = ((f32[16,24,1024]{2,1,0:T(8,128)}), f32[16,24,1024]{2,1,0:T(8,128)S(1)}, u32[]{:S(2)}, u32[]{:S(2)}) async-start(f32[16,24,1024]{2,1,0:T(8,128)} %bitcast.75), calls=%async_computation.3 | async-start | bytes 3145728 | tf_op jit(solution)/shard_map/all_to_all | solution.py:41
  89.0 91.1 %all-gather.2.cloned.1.call-start = ((), (), s32[]{:S(2)}) async-start(), calls=%async_computation.9 | async-start | bytes 1081344 | tf_op jit(solution)/shard_map/all_gather | solution.py:94
  129.0 53.0 %all-to-all-start.4 = ((f32[16,512,32]{1,2,0:T(8,128)}), f32[16,512,32]{1,2,0:T(8,128)S(1)}, u32[]{:S(2)}, u32[]{:S(2)}) async-start(f32[16,512,32]{1,2,0:T(8,128)} %bitcast.19), calls=%async_computation.4 | async-start | bytes 2097152 | tf_op jit(solution)/shard_map/all_to_all | solution.py:41
  136.1 52.7 %copy-start.1 = (f32[2,24,512]{2,1,0:T(8,128)S(1)}, f32[2,24,512]{2,1,0:T(8,128)}, u32[]{:S(2)}) copy-start(f32[2,24,512]{2,1,0:T(8,128)} %param.6) | copy-start | bytes 294916
  183.0 15.6 %all-to-all-start.5 = ((f32[32,1,512]{2,1,0:T(1,128)}), f32[32,1,512]{2,1,0:T(1,128)S(1)}, u32[]{:S(2)}, u32[]{:S(2)}) async-start(f32[32,1,512]{2,1,0:T(1,128)} %reshape.94), calls=%async_computation.5 | async-start | bytes 131072 | tf_op jit(solution)/shard_map/all_to_all | solution.py:41
  200.8 15.8 %all-to-all-start.6 = ((f32[16,1,512]{2,1,0:T(1,128)}), f32[16,1,512]{2,1,0:T(1,128)S(1)}, u32[]{:S(2)}, u32[]{:S(2)}) async-start(f32[16,1,512]{2,1,0:T(1,128)} %reshape.96), calls=%async_computation.6 | async-start | bytes 65536 | tf_op jit(solution)/shard_map/all_to_all | solution.py:47
  220.6 28.1 %all-to-all-start.7 = ((f32[16,512,32]{1,2,0:T(8,128)}), f32[16,512,32]{1,2,0:T(8,128)S(1)}, u32[]{:S(2)}, u32[]{:S(2)}) async-start(f32[16,512,32]{1,2,0:T(8,128)} %bitcast.28), calls=%async_computation.7 | async-start | bytes 2097152 | tf_op jit(solution)/shard_map/all_to_all | solution.py:41
  249.7 18.7 %all-to-all-start.8 = ((f32[32,1,512]{2,1,0:T(1,128)}), f32[32,1,512]{2,1,0:T(1,128)S(1)}, u32[]{:S(2)}, u32[]{:S(2)}) async-start(f32[32,1,512]{2,1,0:T(1,128)} %reshape.98), calls=%async_computation.8 | async-start | bytes 131072 | tf_op jit(solution)/shard_map/all_to_all | solution.py:41
Sparse Core Ops, SparseCore 0:
  93.2 86.8 all-gather.1
